TPU v7x, 32 devices: a whole 2x2x4 slice. The times are simulated.
32 devices in a mesh: sub: 8 (over z, x), fdr: 4 (over y, core).
Axes of the slice: x: 2, y: 2, z: 4, core: 2. Of those that a mesh axis runs over, the one named last changes fastest.
Arguments:
- inverse: bfloat16 [1024, 256, 256], P(('sub', 'fdr')), may hold values from -1 to 1
- cost: float32 [1024, 256, 128], P(('sub', 'fdr')), may hold values from -6 to 6
- lower_limit: float32 [1024, 256], P(('sub', 'fdr')), may hold values from -1.5 to -0.5
- upper_limit: float32 [1024, 256], P(('sub', 'fdr')), may hold values from 0.5 to 1.5
- iface_rows: int32 [1024, 6], P(('sub', 'fdr')), may hold values from 0 to 255, as said below
- substation_of: int32 [1024], P(('sub', 'fdr')), may hold values from 0 to 255, as said below
- live_count: int32 [32], P(('sub', 'fdr')), may hold values from 16 to 32
- reserve_weight: float32 [256], P('sub'), may hold values from 0.5 to 4
- reserve_target: float32 [256, 6, 128], P('sub'), may hold values from -6 to 6
Outputs:
- duals: float32 [1024, 6, 128], P(('sub', 'fdr'))
- consensus: float32 [256, 6, 128], P('sub')
- residual_norms: float32 [5, 2], replicated
- setpoints: float32 [1024, 256, 128], P(('sub', 'fdr'))
Inputs may be any that keep to these rules, and one draw needn't show every extreme that they name: `iface_rows`: each feeder's 6 interface rows are distinct. `substation_of`: of one device's 32 slots at most 6 hang from substations of one owner block (substations k * 32 to k * 32 + 31); for each index of fdr some block gets exactly 6 slots from every device with that index. `live_count`: a device's live feeders fill its first slots; the other slots hold unused data.
All inputs are finite; a program needn't handle non-finite values.
Results may differ from a plain program's by a relative error of at most 0.0069.
Values sent between devices are 32-bit elements; how exact they have to be, the bound alone decides.
No kernel may reach another device: no remote copies, remote signals or barrier semaphores. Data moves between devices by JAX's collectives and lax.ppermute only.
A program may use at most 128 MiB of HBM per device.

v0:
```python
import jax
import jax.numpy as jnp
from jax import lax
from jax.sharding import PartitionSpec as P

ITERS = 5
penalty = 2.0


def shards(
    inverse,
    cost,
    lower_limit,
    upper_limit,
    iface_rows,
    substation_of,
    live_count,
    reserve_weight,
    reserve_target,
):
    slot_count = inverse.shape[0]
    iface_count = iface_rows.shape[1]
    scenarios = cost.shape[2]
    flat_width = iface_count * scenarios
    sub_count = lax.axis_size("sub")
    owned_count = reserve_weight.shape[0]
    total_sub = owned_count * sub_count
    sub_index = lax.axis_index("sub")
    fdr_index = lax.axis_index("fdr")
    active = (jnp.arange(slot_count, dtype=jnp.int32) < live_count[0]).astype(jnp.float32)
    membership = (substation_of[:, None] == jnp.arange(total_sub, dtype=jnp.int32)[None, :]).astype(
        jnp.float32
    ) * active[:, None]
    tallied = lax.psum(jnp.sum(membership, axis=0), ("sub", "fdr"))
    flat_target = reserve_target.reshape(owned_count, flat_width)
    first_row = sub_index * owned_count
    dual_mask = (fdr_index == 0).astype(jnp.float32)
    overflow = max(1, slot_count // (2 * sub_count))
    capacity = max(2, slot_count // sub_count + overflow)
    slot_total = sub_count * capacity
    group_of = substation_of // owned_count
    group_hot = (group_of[:, None] == jnp.arange(sub_count, dtype=jnp.int32)[None, :]).astype(
        jnp.int32
    )
    earlier = jnp.cumsum(group_hot, axis=0) - group_hot
    slot_rank = jnp.sum(earlier * group_hot, axis=1)
    position = group_of * capacity + slot_rank
    slot_match = position[:, None] == jnp.arange(slot_total, dtype=jnp.int32)[None, :]
    slot_hot = slot_match.astype(jnp.float32)
    slot_ids = jnp.sum(slot_match.astype(jnp.int32) * (substation_of + 1)[:, None], axis=0) - 1
    arrived_ids = lax.all_to_all(slot_ids, "sub", split_axis=0, concat_axis=0, tiled=True)
    arrived_hot = (
        (arrived_ids - sub_index * owned_count)[:, None]
        == jnp.arange(owned_count, dtype=jnp.int32)[None, :]
    ).astype(jnp.float32)
    own_members = lax.dynamic_slice_in_dim(tallied, first_row, owned_count, 0)
    feeder_index = jnp.arange(slot_count, dtype=jnp.int32)[:, None]
    scaled_dual = jnp.zeros((slot_count, iface_count, scenarios), jnp.float32)
    local_consensus = jnp.zeros((slot_count, iface_count, scenarios), jnp.float32)
    anchor = jnp.zeros((slot_count, inverse.shape[1], scenarios), jnp.float32)
    old_rows = jnp.zeros((owned_count, flat_width), jnp.float32)
    sums_list = []
    for iteration in range(ITERS):
        right_side = (
            (anchor - cost)
            .at[feeder_index, iface_rows]
            .add(penalty * (local_consensus - scaled_dual))
            .astype(jnp.bfloat16)
        )
        primal = jnp.einsum("fkj,fjs->fks", inverse, right_side, preferred_element_type=jnp.float32)
        anchor = jnp.clip(primal, lower_limit[:, :, None], upper_limit[:, :, None])
        boundary = jnp.take_along_axis(primal, iface_rows[:, :, None], axis=1)
        outgoing = ((boundary + scaled_dual) * active[:, None, None]).reshape(
            slot_count, flat_width
        )
        packed = jnp.einsum("fn,fc->nc", slot_hot, outgoing, precision=lax.Precision.HIGHEST)
        arrived = lax.all_to_all(packed, "sub", split_axis=0, concat_axis=0, tiled=True)
        block_sums = jnp.einsum("no,nc->oc", arrived_hot, arrived, precision=lax.Precision.HIGHEST)
        collected = lax.psum(block_sums, "fdr")
        new_rows = (collected + reserve_weight[:, None] * flat_target) / (
            own_members + reserve_weight
        )[:, None]
        dual_local = dual_mask * jnp.sum(own_members[:, None] * (new_rows - old_rows) ** 2)
        old_rows = new_rows
        reply = jnp.einsum("no,oc->nc", arrived_hot, new_rows, precision=lax.Precision.HIGHEST)
        returned = lax.all_to_all(reply, "sub", split_axis=0, concat_axis=0, tiled=True)
        local_consensus = jnp.einsum(
            "fn,nc->fc", slot_hot, returned, precision=lax.Precision.HIGHEST
        ).reshape(slot_count, iface_count, scenarios)
        mismatch = boundary - local_consensus
        scaled_dual = (scaled_dual + mismatch) * active[:, None, None]
        primal_local = jnp.sum(active[:, None, None] * mismatch**2)
        primal_sum, dual_sum = lax.psum((primal_local, dual_local), ("sub", "fdr"))
        sums_list.append(jnp.stack([primal_sum, dual_sum]))
    stacked = jnp.stack(sums_list)
    residual_norms = jnp.sqrt(stacked) * jnp.array([1.0, penalty], jnp.float32)[None, :]
    consensus = old_rows.reshape(owned_count, iface_count, scenarios)
    return (penalty * scaled_dual, consensus, residual_norms, anchor * active[:, None, None])


def solution(mesh):
    placed = (
        P(("sub", "fdr"), None, None),
        P(("sub", "fdr"), None, None),
        P(("sub", "fdr"), None),
        P(("sub", "fdr"), None),
        P(("sub", "fdr"), None),
        P(("sub", "fdr")),
        P(("sub", "fdr")),
        P("sub"),
        P("sub", None, None),
    )
    return jax.shard_map(
        shards,
        mesh=mesh,
        in_specs=placed,
        out_specs=(
            P(("sub", "fdr"), None, None),
            P("sub", None, None),
            P(),
            P(("sub", "fdr"), None, None),
        ),
        check_vma=False,
    )
```

profile of v0, /device:TPU:0, one launch (start us, length us, event | category | flops | bytes accessed | tf_op | source)
XLA Modules:
  0.0 613.0 jit_solution(17046164565639930385)
XLA Ops:
  9.0 7.3 %all-to-all-start = ((s32[8,6,1]{1,2,0:T(1,128)}), s32[8,6,1]{1,2,0:T(1,128)S(1)}, u32[]{:S(2)}, u32[]{:S(2)}) async-start(s32[8,6,1]{1,2,0:T(1,128)} %bitcast.5), calls=%async_computation | async-start | bytes 8192 | tf_op jit(solution)/shard_map/all_to_all | solution.py:51
  17.7 5.6 copy.151
  23.3 4.6 broadcast_subtract_fusion
  29.0 20.0 %scatter_fusion = f32[32,256,128]{2,1,0:T(8,128)} fusion(f32[32,256,128]{2,1,0:T(8,128)} %broadcast_subtract_fusion, s32[192]{0:T(256)S(1)} %reshape.165, f32[192,128]{1,0:T(8,128)S(1)} %broadcast.263), kind=kCustom, calls=%fused_computation.5 | custom fusion | flops 24576 | bytes 296448 | tf_op jit(solution)/shard_map/scatter-add | solution.py:67
  49.1 9.3 %minimum_subtract_fusion.3 = (f32[32,256,128]{1,2,0:T(8,128)}, f32[32,256,128]{1,2,0:T(8,128)}) fusion(f32[32,256,128]{1,2,0:T(8,128)} %copy.151, f32[32,256]{1,0:T(8,128)S(1)} %copy-done.1, f32[32,256]{1,0:T(8,128)S(1)} %copy-done.2, bf16[32,256,256]{2,1,0:T(8,128)(2,1)} %param.12, f32[32,256,128]{2,1,0:T(8,128)} %scatter_fusion), kind=kOutput, calls=%fused_computation.14 | convolution fusion | flops 541065216 | bytes 21037056 | tf_op jit(solution)/shard_map/fkj,fjs->fks/dot_general | solution.py:70
  58.4 5.6 copy.144
  64.0 4.6 gather_fusion
  68.8 0.9 fusion.42
  69.7 6.0 all-to-all-start.1
  75.9 40.7 %psum.113 = f32[256]{0:T(256)S(1)} all-reduce(f32[256]{0:T(256)S(1)} %select_reduce_fusion), channel_id=1, replica_groups=mesh['sub'=8,'fdr'=4] {'sub','fdr'}, use_global_device_ids=true, to_apply=%region_6.8 | all-reduce | flops 256 | bytes 2048 | tf_op jit(solution)/shard_map/psum | solution.py:34
  116.7 0.9 fusion.33
  117.8 31.6 %all-reduce.7.cloned.1.call-done = f32[32,768]{1,0:T(8,128)} async-done(((f32[32,768]{1,0:T(8,128)}), f32[32,768]{1,0:T(8,128)}) %all-reduce.7.cloned.1.call-update) | async-done | bytes 98320 | tf_op jit(solution)/shard_map/psum | solution.py:79
  149.4 1.0 add_divide_fusion.4
  151.4 5.5 all-to-all-start.2
  156.9 5.6 copy.153
  162.5 2.2 all-to-all-done.2
  165.0 19.9 %scatter_fusion.1 = f32[32,256,128]{2,1,0:T(8,128)} fusion(f32[32,256,128]{2,1,0:T(8,128)} %copy.153, s32[192]{0:T(256)S(1)} %reshape.165, f32[192,128]{1,0:T(8,128)S(1)} %reshape.173), kind=kCustom, calls=%fused_computation.6 | custom fusion | flops 24576 | bytes 296448 | tf_op jit(solution)/shard_map/scatter-add | solution.py:67
  184.9 9.4 %minimum_subtract_fusion.2 = (f32[32,256,128]{1,2,0:T(8,128)}, f32[32,256,128]{1,2,0:T(8,128)}) fusion(f32[32,256,128]{1,2,0:T(8,128)} %copy.151, f32[32,256]{1,0:T(8,128)S(1)} %copy-done.1, f32[32,256]{1,0:T(8,128)S(1)} %copy-done.2, bf16[32,256,256]{2,1,0:T(8,128)(2,1)} %param.12, f32[32,256,128]{2,1,0:T(8,128)} %scatter_fusion.1), kind=kOutput, calls=%fused_computation.13 | convolution fusion | flops 541065216 | bytes 21037056 | tf_op jit(solution)/shard_map/fkj,fjs->fks/dot_general | solution.py:70
  194.3 5.6 copy.156
  199.8 4.6 gather_fusion.1
  204.9 11.5 %all_to_all.111 = f32[8,6,768]{2,1,0:T(8,128)S(1)} all-to-all(f32[8,6,768]{2,1,0:T(8,128)S(1)} %fusion.40), channel_id=1, replica_groups=mesh['sub'=8,'fdr'=4] {'sub'}, dimensions={0} | all-to-all | bytes 294912 | tf_op jit(solution)/shard_map/all_to_all | solution.py:77
  216.4 0.9 fusion.31
  217.4 29.0 %all-reduce.9.cloned.1.call-done = f32[32,768]{1,0:T(8,128)} async-done(((f32[32,768]{1,0:T(8,128)}), f32[32,768]{1,0:T(8,128)}) %all-reduce.9.cloned.1.call-update) | async-done | bytes 98320 | tf_op jit(solution)/shard_map/psum | solution.py:79
  246.3 1.0 add_divide_fusion.3
  248.3 5.5 all-to-all-start.4
  253.9 5.6 copy.163
  259.4 2.2 all-to-all-done.4
  262.0 19.9 %scatter_fusion.2 = f32[32,256,128]{2,1,0:T(8,128)} fusion(f32[32,256,128]{2,1,0:T(8,128)} %copy.163, s32[192]{0:T(256)S(1)} %reshape.165, f32[192,128]{1,0:T(8,128)S(1)} %reshape.179), kind=kCustom, calls=%fused_computation.7 | custom fusion | flops 24576 | bytes 296448 | tf_op jit(solution)/shard_map/scatter-add | solution.py:67
  281.8 9.4 %minimum_subtract_fusion.1 = (f32[32,256,128]{1,2,0:T(8,128)}, f32[32,256,128]{1,2,0:T(8,128)}) fusion(f32[32,256,128]{1,2,0:T(8,128)} %copy.151, f32[32,256]{1,0:T(8,128)S(1)} %copy-done.1, f32[32,256]{1,0:T(8,128)S(1)} %copy-done.2, bf16[32,256,256]{2,1,0:T(8,128)(2,1)} %param.12, f32[32,256,128]{2,1,0:T(8,128)} %scatter_fusion.2), kind=kOutput, calls=%fused_computation.12 | convolution fusion | flops 541065216 | bytes 21037056 | tf_op jit(solution)/shard_map/fkj,fjs->fks/dot_general | solution.py:70
  291.2 5.6 copy.166
  296.8 4.6 gather_fusion.2
  301.8 11.5 %all_to_all.112 = f32[8,6,768]{2,1,0:T(8,128)S(1)} all-to-all(f32[8,6,768]{2,1,0:T(8,128)S(1)} %fusion.38), channel_id=1, replica_groups=mesh['sub'=8,'fdr'=4] {'sub'}, dimensions={0} | all-to-all | bytes 294912 | tf_op jit(solution)/shard_map/all_to_all | solution.py:77
  313.4 0.9 fusion.29
  314.3 28.9 %all-reduce.11.cloned.1.call-done = f32[32,768]{1,0:T(8,128)} async-done(((f32[32,768]{1,0:T(8,128)}), f32[32,768]{1,0:T(8,128)}) %all-reduce.11.cloned.1.call-update) | async-done | bytes 98320 | tf_op jit(solution)/shard_map/psum | solution.py:79
  343.3 1.0 add_divide_fusion.2
  345.2 5.5 all-to-all-start.6
  350.8 5.6 copy.173
  356.4 2.2 all-to-all-done.6
  358.9 19.9 %scatter_fusion.3 = f32[32,256,128]{2,1,0:T(8,128)} fusion(f32[32,256,128]{2,1,0:T(8,128)} %copy.173, s32[192]{0:T(256)S(1)} %reshape.165, f32[192,128]{1,0:T(8,128)S(1)} %reshape.185), kind=kCustom, calls=%fused_computation.8 | custom fusion | flops 24576 | bytes 296448 | tf_op jit(solution)/shard_map/scatter-add | solution.py:67
  378.8 9.6 %minimum_subtract_fusion = (f32[32,256,128]{1,2,0:T(8,128)}, f32[32,256,128]{1,2,0:T(8,128)}) fusion(f32[32,256,128]{1,2,0:T(8,128)} %copy.151, f32[32,256]{1,0:T(8,128)S(1)} %copy-done.1, f32[32,256]{1,0:T(8,128)S(1)} %copy-done.2, bf16[32,256,256]{2,1,0:T(8,128)(2,1)} %param.12, f32[32,256,128]{2,1,0:T(8,128)} %scatter_fusion.3), kind=kOutput, calls=%fused_computation.11 | convolution fusion | flops 541065216 | bytes 21037056 | tf_op jit(solution)/shard_map/fkj,fjs->fks/dot_general | solution.py:70
  388.3 5.6 copy.176
  393.9 4.6 gather_fusion.3
  398.9 11.5 %all_to_all.113 = f32[8,6,768]{2,1,0:T(8,128)S(1)} all-to-all(f32[8,6,768]{2,1,0:T(8,128)S(1)} %fusion.36), channel_id=1, replica_groups=mesh['sub'=8,'fdr'=4] {'sub'}, dimensions={0} | all-to-all | bytes 294912 | tf_op jit(solution)/shard_map/all_to_all | solution.py:77
  410.5 0.9 fusion.27
  411.4 28.9 %all-reduce.13.cloned.1.call-done = f32[32,768]{1,0:T(8,128)} async-done(((f32[32,768]{1,0:T(8,128)}), f32[32,768]{1,0:T(8,128)}) %all-reduce.13.cloned.1.call-update) | async-done | bytes 98320 | tf_op jit(solution)/shard_map/psum | solution.py:79
  440.4 1.0 add_divide_fusion.1
  442.3 5.5 all-to-all-start.8
  448.1 5.6 copy.183
  453.7 1.9 all-to-all-done.8
  456.0 19.9 %scatter_fusion.4 = f32[32,256,128]{2,1,0:T(8,128)} fusion(f32[32,256,128]{2,1,0:T(8,128)} %copy.183, s32[192]{0:T(256)S(1)} %reshape.165, f32[192,128]{1,0:T(8,128)S(1)} %reshape.191), kind=kCustom, calls=%fused_computation.9 | custom fusion | flops 24576 | bytes 296448 | tf_op jit(solution)/shard_map/scatter-add | solution.py:67
  475.9 8.4 %minimum_multiply_fusion = (f32[32,256,128]{1,2,0:T(8,128)}, f32[32,256,128]{1,2,0:T(8,128)}) fusion(f32[32]{0:T(128)S(1)} %compare_convert_fusion, f32[32,256]{1,0:T(8,128)S(1)} %copy-done.1, f32[32,256]{1,0:T(8,128)S(1)} %copy-done.2, bf16[32,256,256]{2,1,0:T(8,128)(2,1)} %param.12, f32[32,256,128]{2,1,0:T(8,128)} %scatter_fusion.4), kind=kOutput, calls=%fused_computation.10 | convolution fusion | flops 541065216 | bytes 16842880 | tf_op jit(solution)/shard_map/fkj,fjs->fks/dot_general | solution.py:70
  484.2 5.6 copy.186
  489.8 4.6 gather_fusion.4
  494.8 11.5 %all_to_all.114 = f32[8,6,768]{2,1,0:T(8,128)S(1)} all-to-all(f32[8,6,768]{2,1,0:T(8,128)S(1)} %fusion.34), channel_id=1, replica_groups=mesh['sub'=8,'fdr'=4] {'sub'}, dimensions={0} | all-to-all | bytes 294912 | tf_op jit(solution)/shard_map/all_to_all | solution.py:77
  506.4 0.9 fusion.25
  507.4 28.9 %all-reduce.15.cloned.1.call-done = f32[32,768]{1,0:T(8,128)} async-done(((f32[32,768]{1,0:T(8,128)}), f32[32,768]{1,0:T(8,128)}) %all-reduce.15.cloned.1.call-update) | async-done | bytes 98320 | tf_op jit(solution)/shard_map/psum | solution.py:79
  536.3 1.7 multiply_reduce_fusion
  539.0 5.5 all-to-all-start.10
  544.5 5.6 copy.197
  554.0 1.6 multiply_reduce_fusion.1
  555.6 43.2 %all-reduce = (f32[1]{0:T(128)}, f32[1]{0:T(128)}, f32[1]{0:T(128)}, f32[1]{0:T(128)}, f32[1]{0:T(128)}, /*index=5*/f32[1]{0:T(128)}, f32[1]{0:T(128)}, f32[1]{0:T(128)}, f32[1]{0:T(128)}, f32[1]{0:T(128)}) all-reduce(f32[1]{0:T(128)} %bitcast.21, f32[1]{0:T(128)} %bitcast.20, ...), channel_id=1, replica_groups=mesh['sub'=8,'fdr'=4] {'sub','fdr'}, use_global_device_ids=true, to_apply=%region_18.20 | all-reduce | flops 10 | bytes 80 | tf_op jit(solution)/shard_map/psum | solution.py:93
  598.7 2.6 maximum_bitcast_fusion
  601.5 1.4 maximum_bitcast_fusion.4
  603.0 2.5 maximum_bitcast_fusion.2
  (111 shorter events, 14.5 us)
Async XLA Ops:
  7.2 142.3 %copy-start = (f32[32,6,128]{2,0,1:T(8,128)S(1)}, f32[32,6,128]{2,0,1:T(8,128)}, u32[]{:S(2)}) copy-start(f32[32,6,128]{2,0,1:T(8,128)} %param.20) | copy-start | bytes 294916
  9.0 60.7 %all-to-all-start = ((s32[8,6,1]{1,2,0:T(1,128)}), s32[8,6,1]{1,2,0:T(1,128)S(1)}, u32[]{:S(2)}, u32[]{:S(2)}) async-start(s32[8,6,1]{1,2,0:T(1,128)} %bitcast.5), calls=%async_computation | async-start | bytes 8192 | tf_op jit(solution)/shard_map/all_to_all | solution.py:51
  23.3 25.8 %copy-start.1 = (f32[32,256]{1,0:T(8,128)S(1)}, f32[32,256]{1,0:T(8,128)}, u32[]{:S(2)}) copy-start(f32[32,256]{1,0:T(8,128)} %param.14) | copy-start | bytes 98308
  23.3 25.8 %copy-start.2 = (f32[32,256]{1,0:T(8,128)S(1)}, f32[32,256]{1,0:T(8,128)}, u32[]{:S(2)}) copy-start(f32[32,256]{1,0:T(8,128)} %param.15) | copy-start | bytes 98308
  58.4 17.4 %copy-start.5 = (s32[32]{0:T(128)S(1)}, s32[32]{0:T(128)}, u32[]{:S(2)}) copy-start(s32[32]{0:T(128)} %param.17) | copy-start | bytes 388
  58.4 59.3 %copy-start.3 = (f32[32]{0:T(128)S(1)}, f32[32]{0:T(128)}, u32[]{:S(2)}) copy-start(f32[32]{0:T(128)} %param.19) | copy-start | bytes 388
  69.7 47.0 %all-to-all-start.1 = ((f32[8,6,768]{2,1,0:T(8,128)}), f32[8,6,768]{2,1,0:T(8,128)S(1)}, u32[]{:S(2)}, u32[]{:S(2)}) async-start(f32[8,6,768]{2,1,0:T(8,128)} %fusion.42), calls=%async_computation.1 | async-start | bytes 393216 | tf_op jit(solution)/shard_map/all_to_all | solution.py:77
  75.7 73.7 %all-reduce.7.cloned.1.call-start = ((), (), s32[]{:S(2)}) async-start(), calls=%async_computation.11 | async-start | bytes 196608 | tf_op jit(solution)/shard_map/psum | solution.py:79
  151.4 13.3 %all-to-all-start.2 = ((f32[8,6,768]{2,1,0:T(8,128)}), f32[8,6,768]{2,1,0:T(8,128)S(1)}, u32[]{:S(2)}, u32[]{:S(2)}) async-start(f32[8,6,768]{2,1,0:T(8,128)} %all_to_all.77), calls=%async_computation.2 | async-start | bytes 393216 | tf_op jit(solution)/shard_map/all_to_all | solution.py:86
  156.9 89.5 %all-reduce.9.cloned.1.call-start = ((), (), s32[]{:S(2)}) async-start(), calls=%async_computation.12 | async-start | bytes 196608 | tf_op jit(solution)/shard_map/psum | solution.py:79
  248.3 13.3 %all-to-all-start.4 = ((f32[8,6,768]{2,1,0:T(8,128)}), f32[8,6,768]{2,1,0:T(8,128)S(1)}, u32[]{:S(2)}, u32[]{:S(2)}) async-start(f32[8,6,768]{2,1,0:T(8,128)} %all_to_all.82), calls=%async_computation.4 | async-start | bytes 393216 | tf_op jit(solution)/shard_map/all_to_all | solution.py:86
  253.8 89.5 %all-reduce.11.cloned.1.call-start = ((), (), s32[]{:S(2)}) async-start(), calls=%async_computation.13 | async-start | bytes 196608 | tf_op jit(solution)/shard_map/psum | solution.py:79
  345.2 13.3 %all-to-all-start.6 = ((f32[8,6,768]{2,1,0:T(8,128)}), f32[8,6,768]{2,1,0:T(8,128)S(1)}, u32[]{:S(2)}, u32[]{:S(2)}) async-start(f32[8,6,768]{2,1,0:T(8,128)} %all_to_all.87), calls=%async_computation.6 | async-start | bytes 393216 | tf_op jit(solution)/shard_map/all_to_all | solution.py:86
  350.7 89.7 %all-reduce.13.cloned.1.call-start = ((), (), s32[]{:S(2)}) async-start(), calls=%async_computation.14 | async-start | bytes 196608 | tf_op jit(solution)/shard_map/psum | solution.py:79
  442.3 13.3 %all-to-all-start.8 = ((f32[8,6,768]{2,1,0:T(8,128)}), f32[8,6,768]{2,1,0:T(8,128)S(1)}, u32[]{:S(2)}, u32[]{:S(2)}) async-start(f32[8,6,768]{2,1,0:T(8,128)} %all_to_all.92), calls=%async_computation.8 | async-start | bytes 393216 | tf_op jit(solution)/shard_map/all_to_all | solution.py:86
  447.8 88.5 %all-reduce.15.cloned.1.call-start = ((), (), s32[]{:S(2)}) async-start(), calls=%async_computation.15 | async-start | bytes 196608 | tf_op jit(solution)/shard_map/psum | solution.py:79
  539.0 15.0 %all-to-all-start.10 = ((f32[8,6,768]{2,1,0:T(8,128)}), f32[8,6,768]{2,1,0:T(8,128)S(1)}, u32[]{:S(2)}, u32[]{:S(2)}) async-start(f32[8,6,768]{2,1,0:T(8,128)} %all_to_all.97), calls=%async_computation.10 | async-start | bytes 393216 | tf_op jit(solution)/shard_map/all_to_all | solution.py:86
  544.5 61.3 %copy-start.4 = (f32[2]{0:T(128)S(1)}, f32[2]{0:T(128)}, u32[]{:S(2)}) copy-start(f32[2]{0:T(128)} %constant.68.clone) | copy-start | bytes 28
Sparse Core Ops, SparseCore 0:
  117.8 31.5 all-reduce.6
  217.5 28.7 all-reduce.8
  314.4 28.7 all-reduce.10
  411.6 28.7 all-reduce.12
  507.5 28.7 all-reduce.14
where the time goes:
time: 617 us; the launch traced here: 613 us
  waiting for transfers between devices  156 us (25%)
  blocking collectives  130 us (21%)
  other arithmetic  120 us (19%)
  local copies, waits for them, and re-layouts  91.1 us (15%)
  matrix products  56.4 us (9%)
  starting transfers between devices  41.3 us (7%)
  between operations  18.1 us (3%)
    psum x5, waiting for transfers between devices, shards(): collected = lax.psum(block_sums, 'fdr')  147 us
    scatter-add x5, other arithmetic, shards(): right_side = (anchor - cost).at[feeder_index, iface_rows].add(penalty * (...  99.5 us
    all_to_all x4, blocking collectives, shards(): lax.all_to_all(packed, 'sub', split_axis=0, concat_axis=0, tiled=True)  46.1 us
    dot_general x5, matrix products, shards(): jnp.einsum('fkj,fjs->fks', inverse, right_side, preferred_element_type=jn...  46 us
    psum x1, blocking collectives, shards(): primal_sum, dual_sum = lax.psum((primal_local, dual_local), ('sub', 'fdr'))  43.2 us
    psum x1, blocking collectives, shards(): tallied = lax.psum(jnp.sum(membership, axis=0), ('sub', 'fdr'))  40.7 us
    dot_general x5, local copies, waits for them, and re-layouts, shards(): jnp.einsum('fkj,fjs->fks', inverse, right_side, preferred_element_type=jn...  27.9 us
    all_to_all x5, starting transfers between devices, shards(): lax.all_to_all(reply, 'sub', split_axis=0, concat_axis=0, tiled=True)  27.6 us
  transfers between devices with their start and end apart: 12, of which 9 were waited for; matrix products, arithmetic and copies ran while one was open for 13% of the time, Pallas kernels for 0%

commit v1 on v0

--- a/solution.py
+++ b/solution.py
@@ -76,7 +76,11 @@
         packed = jnp.einsum("fn,fc->nc", slot_hot, outgoing, precision=lax.Precision.HIGHEST)
         arrived = lax.all_to_all(packed, "sub", split_axis=0, concat_axis=0, tiled=True)
         block_sums = jnp.einsum("no,nc->oc", arrived_hot, arrived, precision=lax.Precision.HIGHEST)
-        collected = lax.psum(block_sums, "fdr")
+        collected = block_sums
+        for hop in (1, 2):
+            collected = collected + lax.ppermute(
+                collected, "fdr", [(dev, dev ^ hop) for dev in range(4)]
+            )
         new_rows = (collected + reserve_weight[:, None] * flat_target) / (
             own_members + reserve_weight
         )[:, None]

time: 617 us -> 475 us (0.77)
  waiting for transfers between devices: 156 us -> 39.7 us
  between operations: 18.1 us -> 5.09 us
    psum x5 -> x0, waiting for transfers between devices: 147 us -> none  [shards(): collected = lax.psum(block_sums, 'fdr')]
    ppermute x0 -> x10, waiting for transfers between devices: none -> 23.6 us  [shards(): lax.ppermute(collected, 'fdr', [(dev, dev ^ hop) for dev in range(4)])]
    all_to_all x5, starting transfers between devices: 27.6 us -> 18.2 us  [shards(): lax.all_to_all(reply, 'sub', split_axis=0, concat_axis=0, tiled=True)]
    all_to_all x1, waiting for transfers between devices: 0.01 us -> 7.68 us  [shards(): lax.all_to_all(packed, 'sub', split_axis=0, concat_axis=0, tiled=True)]
    ppermute x0 -> x10, starting transfers between devices: none -> 6.4 us  [shards(): lax.ppermute(collected, 'fdr', [(dev, dev ^ hop) for dev in range(4)])]
  transfers between devices with their start and end apart: 12 -> 17, of which waited for: 9 -> 14; matrix products, arithmetic and copies ran while one was open for 13% -> 17% of each run, Pallas kernels for 0% -> 0%
where the time goes in v1:
time: 475 us; the launch traced here: 471 us
  blocking collectives  128 us (27%)
  other arithmetic  116 us (24%)
  local copies, waits for them, and re-layouts  91.1 us (19%)
  matrix products  53.2 us (11%)
  waiting for transfers between devices  39.7 us (8%)
  starting transfers between devices  37.9 us (8%)
  between operations  5.09 us (1%)
    scatter-add x5, other arithmetic, shards(): right_side = (anchor - cost).at[feeder_index, iface_rows].add(penalty * (...  99.5 us
    all_to_all x4, blocking collectives, shards(): lax.all_to_all(packed, 'sub', split_axis=0, concat_axis=0, tiled=True)  46.1 us
    dot_general x5, matrix products, shards(): jnp.einsum('fkj,fjs->fks', inverse, right_side, preferred_element_type=jn...  46 us
    psum x1, blocking collectives, shards(): primal_sum, dual_sum = lax.psum((primal_local, dual_local), ('sub', 'fdr'))  43.3 us
    psum x1, blocking collectives, shards(): tallied = lax.psum(jnp.sum(membership, axis=0), ('sub', 'fdr'))  38.6 us
    dot_general x5, local copies, waits for them, and re-layouts, shards(): jnp.einsum('fkj,fjs->fks', inverse, right_side, preferred_element_type=jn...  27.9 us
    ppermute x10, waiting for transfers between devices, shards(): lax.ppermute(collected, 'fdr', [(dev, dev ^ hop) for dev in range(4)])  23.6 us
    gather x12, local copies, waits for them, and re-layouts, shards(): boundary = jnp.take_along_axis(primal, iface_rows[:, :, None], axis=1)  23 us
  transfers between devices with their start and end apart: 17, of which 14 were waited for; matrix products, arithmetic and copies ran while one was open for 17% of the time, Pallas kernels for 0%

profile of v1, /device:TPU:0, one launch (start us, length us, event | category | flops | bytes accessed | tf_op | source)
XLA Modules:
  0.0 470.7 jit_solution(7262412601604034130)
XLA Ops:
  2.5 7.3 %all-to-all-start = ((s32[8,6,1]{1,2,0:T(1,128)}), s32[8,6,1]{1,2,0:T(1,128)S(1)}, u32[]{:S(2)}, u32[]{:S(2)}) async-start(s32[8,6,1]{1,2,0:T(1,128)} %bitcast.5), calls=%async_computation | async-start | bytes 8192 | tf_op jit(solution)/shard_map/all_to_all | solution.py:51
  11.1 5.6 %copy.151 = f32[32,256,128]{1,2,0:T(8,128)} copy(f32[32,256,128]{2,1,0:T(8,128)} %param.13) | data formatting | bytes 8388608 | tf_op args[1]
  16.7 4.6 broadcast_subtract_fusion
  22.5 20.0 %scatter_fusion = f32[32,256,128]{2,1,0:T(8,128)} fusion(f32[32,256,128]{2,1,0:T(8,128)} %broadcast_subtract_fusion, s32[192]{0:T(256)S(1)} %reshape.165, f32[192,128]{1,0:T(8,128)S(1)} %broadcast.263), kind=kCustom, calls=%fused_computation.5 | custom fusion | flops 24576 | bytes 296448 | tf_op jit(solution)/shard_map/scatter-add | solution.py:67
  42.5 9.3 %minimum_subtract_fusion.3 = (f32[32,256,128]{1,2,0:T(8,128)}, f32[32,256,128]{1,2,0:T(8,128)}) fusion(f32[32,256,128]{1,2,0:T(8,128)} %copy.151, f32[32,256]{1,0:T(8,128)S(1)} %copy-done.1, f32[32,256]{1,0:T(8,128)S(1)} %copy-done.2, bf16[32,256,256]{2,1,0:T(8,128)(2,1)} %param.12, f32[32,256,128]{2,1,0:T(8,128)} %scatter_fusion), kind=kOutput, calls=%fused_computation.14 | convolution fusion | flops 541065216 | bytes 21037056 | tf_op jit(solution)/shard_map/fkj,fjs->fks/dot_general | solution.py:70
  51.9 5.6 %copy.144 = f32[32,256,128]{2,1,0:T(8,128)} copy(f32[32,256,128]{1,2,0:T(8,128)} %get-tuple-element.61) | data formatting | bytes 8388608 | tf_op jit(solution)/shard_map/fkj,fjs->fks/dot_general | solution.py:70
  57.5 4.6 gather_fusion
  62.3 0.9 fusion.42
  63.2 6.0 %all-to-all-start.1 = ((f32[8,6,768]{2,1,0:T(8,128)}), f32[8,6,768]{2,1,0:T(8,128)S(1)}, u32[]{:S(2)}, u32[]{:S(2)}) async-start(f32[8,6,768]{2,1,0:T(8,128)} %fusion.42), calls=%async_computation.1 | async-start | bytes 393216 | tf_op jit(solution)/shard_map/all_to_all | solution.py:77
  69.3 7.7 %all-to-all-done.1 = f32[8,6,768]{2,1,0:T(8,128)S(1)} async-done(((f32[8,6,768]{2,1,0:T(8,128)}), f32[8,6,768]{2,1,0:T(8,128)S(1)}, u32[]{:S(2)}, u32[]{:S(2)}) %all-to-all-start.1) | async-done | bytes 147488 | tf_op jit(solution)/shard_map/all_to_all | solution.py:77
  77.5 38.6 %psum.77 = f32[256]{0:T(256)S(1)} all-reduce(f32[256]{0:T(256)S(1)} %select_reduce_fusion), channel_id=1, replica_groups=mesh['sub'=8,'fdr'=4] {'sub','fdr'}, use_global_device_ids=true, to_apply=%region_5.7 | all-reduce | flops 256 | bytes 2048 | tf_op jit(solution)/shard_map/psum | solution.py:34
  116.1 2.3 collective-permute-start.1
  118.5 2.5 collective-permute-done.1
  122.1 4.4 all-to-all-start.2
  126.5 5.6 %copy.153 = f32[32,256,128]{2,1,0:T(8,128)} copy(f32[32,256,128]{1,2,0:T(8,128)} %get-tuple-element.60) | data formatting | bytes 8388608 | tf_op jit(solution)/shard_map/sub | solution.py:65
  132.1 2.2 all-to-all-done.2
  134.7 19.9 %scatter_fusion.1 = f32[32,256,128]{2,1,0:T(8,128)} fusion(f32[32,256,128]{2,1,0:T(8,128)} %copy.153, s32[192]{0:T(256)S(1)} %reshape.165, f32[192,128]{1,0:T(8,128)S(1)} %reshape.173), kind=kCustom, calls=%fused_computation.6 | custom fusion | flops 24576 | bytes 296448 | tf_op jit(solution)/shard_map/scatter-add | solution.py:67
  154.5 9.4 %minimum_subtract_fusion.2 = (f32[32,256,128]{1,2,0:T(8,128)}, f32[32,256,128]{1,2,0:T(8,128)}) fusion(f32[32,256,128]{1,2,0:T(8,128)} %copy.151, f32[32,256]{1,0:T(8,128)S(1)} %copy-done.1, f32[32,256]{1,0:T(8,128)S(1)} %copy-done.2, bf16[32,256,256]{2,1,0:T(8,128)(2,1)} %param.12, f32[32,256,128]{2,1,0:T(8,128)} %scatter_fusion.1), kind=kOutput, calls=%fused_computation.13 | convolution fusion | flops 541065216 | bytes 21037056 | tf_op jit(solution)/shard_map/fkj,fjs->fks/dot_general | solution.py:70
  163.9 5.6 %copy.156 = f32[32,256,128]{2,1,0:T(8,128)} copy(f32[32,256,128]{1,2,0:T(8,128)} %get-tuple-element.64) | data formatting | bytes 8388608 | tf_op jit(solution)/shard_map/fkj,fjs->fks/dot_general | solution.py:70
  169.5 4.6 gather_fusion.1
  174.5 11.5 %all_to_all.111 = f32[8,6,768]{2,1,0:T(8,128)S(1)} all-to-all(f32[8,6,768]{2,1,0:T(8,128)S(1)} %fusion.40), channel_id=1, replica_groups=mesh['sub'=8,'fdr'=4] {'sub'}, dimensions={0} | all-to-all | bytes 294912 | tf_op jit(solution)/shard_map/all_to_all | solution.py:77
  186.4 1.3 collective-permute-done.2
  187.7 1.1 collective-permute-start.3
  188.8 3.8 collective-permute-done.3
  193.7 3.4 all-to-all-start.4
  197.1 5.6 %copy.163 = f32[32,256,128]{2,1,0:T(8,128)} copy(f32[32,256,128]{1,2,0:T(8,128)} %get-tuple-element.63) | data formatting | bytes 8388608 | tf_op jit(solution)/shard_map/sub | solution.py:65
  202.7 2.1 all-to-all-done.4
  205.2 19.9 %scatter_fusion.2 = f32[32,256,128]{2,1,0:T(8,128)} fusion(f32[32,256,128]{2,1,0:T(8,128)} %copy.163, s32[192]{0:T(256)S(1)} %reshape.165, f32[192,128]{1,0:T(8,128)S(1)} %reshape.179), kind=kCustom, calls=%fused_computation.7 | custom fusion | flops 24576 | bytes 296448 | tf_op jit(solution)/shard_map/scatter-add | solution.py:67
  225.1 9.4 %minimum_subtract_fusion.1 = (f32[32,256,128]{1,2,0:T(8,128)}, f32[32,256,128]{1,2,0:T(8,128)}) fusion(f32[32,256,128]{1,2,0:T(8,128)} %copy.151, f32[32,256]{1,0:T(8,128)S(1)} %copy-done.1, f32[32,256]{1,0:T(8,128)S(1)} %copy-done.2, bf16[32,256,256]{2,1,0:T(8,128)(2,1)} %param.12, f32[32,256,128]{2,1,0:T(8,128)} %scatter_fusion.2), kind=kOutput, calls=%fused_computation.12 | convolution fusion | flops 541065216 | bytes 21037056 | tf_op jit(solution)/shard_map/fkj,fjs->fks/dot_general | solution.py:70
  234.4 5.6 %copy.166 = f32[32,256,128]{2,1,0:T(8,128)} copy(f32[32,256,128]{1,2,0:T(8,128)} %get-tuple-element.67) | data formatting | bytes 8388608 | tf_op jit(solution)/shard_map/fkj,fjs->fks/dot_general | solution.py:70
  240.0 4.6 gather_fusion.2
  245.0 11.5 %all_to_all.112 = f32[8,6,768]{2,1,0:T(8,128)S(1)} all-to-all(f32[8,6,768]{2,1,0:T(8,128)S(1)} %fusion.38), channel_id=1, replica_groups=mesh['sub'=8,'fdr'=4] {'sub'}, dimensions={0} | all-to-all | bytes 294912 | tf_op jit(solution)/shard_map/all_to_all | solution.py:77
  257.0 1.3 collective-permute-done.4
  258.3 1.0 collective-permute-start.5
  259.2 3.9 collective-permute-done.5
  264.2 3.4 all-to-all-start.6
  267.6 5.6 %copy.173 = f32[32,256,128]{2,1,0:T(8,128)} copy(f32[32,256,128]{1,2,0:T(8,128)} %get-tuple-element.66) | data formatting | bytes 8388608 | tf_op jit(solution)/shard_map/sub | solution.py:65
  273.2 2.1 all-to-all-done.6
  275.7 19.9 %scatter_fusion.3 = f32[32,256,128]{2,1,0:T(8,128)} fusion(f32[32,256,128]{2,1,0:T(8,128)} %copy.173, s32[192]{0:T(256)S(1)} %reshape.165, f32[192,128]{1,0:T(8,128)S(1)} %reshape.185), kind=kCustom, calls=%fused_computation.8 | custom fusion | flops 24576 | bytes 296448 | tf_op jit(solution)/shard_map/scatter-add | solution.py:67
  295.6 9.5 %minimum_subtract_fusion = (f32[32,256,128]{1,2,0:T(8,128)}, f32[32,256,128]{1,2,0:T(8,128)}) fusion(f32[32,256,128]{1,2,0:T(8,128)} %copy.151, f32[32,256]{1,0:T(8,128)S(1)} %copy-done.1, f32[32,256]{1,0:T(8,128)S(1)} %copy-done.2, bf16[32,256,256]{2,1,0:T(8,128)(2,1)} %param.12, f32[32,256,128]{2,1,0:T(8,128)} %scatter_fusion.3), kind=kOutput, calls=%fused_computation.11 | convolution fusion | flops 541065216 | bytes 21037056 | tf_op jit(solution)/shard_map/fkj,fjs->fks/dot_general | solution.py:70
  305.2 5.6 %copy.176 = f32[32,256,128]{2,1,0:T(8,128)} copy(f32[32,256,128]{1,2,0:T(8,128)} %get-tuple-element.70) | data formatting | bytes 8388608 | tf_op jit(solution)/shard_map/fkj,fjs->fks/dot_general | solution.py:70
  310.7 4.6 gather_fusion.3
  315.8 11.5 %all_to_all.113 = f32[8,6,768]{2,1,0:T(8,128)S(1)} all-to-all(f32[8,6,768]{2,1,0:T(8,128)S(1)} %fusion.36), channel_id=1, replica_groups=mesh['sub'=8,'fdr'=4] {'sub'}, dimensions={0} | all-to-all | bytes 294912 | tf_op jit(solution)/shard_map/all_to_all | solution.py:77
  327.7 1.3 collective-permute-done.6
  329.0 0.9 collective-permute-start.7
  329.9 4.0 collective-permute-done.7
  335.0 3.6 all-to-all-start.8
  338.6 5.6 %copy.183 = f32[32,256,128]{2,1,0:T(8,128)} copy(f32[32,256,128]{1,2,0:T(8,128)} %get-tuple-element.69) | data formatting | bytes 8388608 | tf_op jit(solution)/shard_map/sub | solution.py:65
  344.2 1.9 all-to-all-done.8
  346.5 19.9 %scatter_fusion.4 = f32[32,256,128]{2,1,0:T(8,128)} fusion(f32[32,256,128]{2,1,0:T(8,128)} %copy.183, s32[192]{0:T(256)S(1)} %reshape.165, f32[192,128]{1,0:T(8,128)S(1)} %reshape.191), kind=kCustom, calls=%fused_computation.9 | custom fusion | flops 24576 | bytes 296448 | tf_op jit(solution)/shard_map/scatter-add | solution.py:67
  366.3 8.4 %minimum_multiply_fusion = (f32[32,256,128]{1,2,0:T(8,128)}, f32[32,256,128]{1,2,0:T(8,128)}) fusion(f32[32]{0:T(128)S(1)} %compare_convert_fusion, f32[32,256]{1,0:T(8,128)S(1)} %copy-done.1, f32[32,256]{1,0:T(8,128)S(1)} %copy-done.2, bf16[32,256,256]{2,1,0:T(8,128)(2,1)} %param.12, f32[32,256,128]{2,1,0:T(8,128)} %scatter_fusion.4), kind=kOutput, calls=%fused_computation.10 | convolution fusion | flops 541065216 | bytes 16842880 | tf_op jit(solution)/shard_map/fkj,fjs->fks/dot_general | solution.py:70
  374.7 5.6 %copy.186 = f32[32,256,128]{2,1,0:T(8,128)} copy(f32[32,256,128]{1,2,0:T(8,128)} %get-tuple-element.72) | data formatting | bytes 8388608 | tf_op jit(solution)/shard_map/fkj,fjs->fks/dot_general | solution.py:70
  380.3 4.6 gather_fusion.4
  385.3 11.5 %all_to_all.114 = f32[8,6,768]{2,1,0:T(8,128)S(1)} all-to-all(f32[8,6,768]{2,1,0:T(8,128)S(1)} %fusion.34), channel_id=1, replica_groups=mesh['sub'=8,'fdr'=4] {'sub'}, dimensions={0} | all-to-all | bytes 294912 | tf_op jit(solution)/shard_map/all_to_all | solution.py:77
  397.2 1.3 collective-permute-done.8
  399.3 4.1 collective-permute-done.9
  403.5 0.8 multiply_reduce_fusion
  405.3 3.4 all-to-all-start.10
  408.7 5.6 %copy.197 = f32[32,256,128]{2,1,0:T(8,128)} copy(f32[32,256,128]{1,2,0:T(8,128)} %get-tuple-element.71) | data formatting | bytes 8388608
  418.1 1.6 multiply_reduce_fusion.1
  419.7 43.3 %all-reduce = (f32[1]{0:T(128)}, f32[1]{0:T(128)}, f32[1]{0:T(128)}, f32[1]{0:T(128)}, f32[1]{0:T(128)}, /*index=5*/f32[1]{0:T(128)}, f32[1]{0:T(128)}, f32[1]{0:T(128)}, f32[1]{0:T(128)}, f32[1]{0:T(128)}) all-reduce(f32[1]{0:T(128)} %bitcast.21, f32[1]{0:T(128)} %bitcast.20, ...), channel_id=1, replica_groups=mesh['sub'=8,'fdr'=4] {'sub','fdr'}, use_global_device_ids=true, to_apply=%region_13.15 | all-reduce | flops 10 | bytes 80 | tf_op jit(solution)/shard_map/psum | solution.py:97
  463.0 2.6 maximum_bitcast_fusion
  465.8 1.4 maximum_bitcast_fusion.4
  467.3 2.5 maximum_bitcast_fusion.2
  (121 shorter events, 17.1 us)
Async XLA Ops:
  0.6 120.4 %copy-start = (f32[32,6,128]{2,0,1:T(8,128)S(1)}, f32[32,6,128]{2,0,1:T(8,128)}, u32[]{:S(2)}) copy-start(f32[32,6,128]{2,0,1:T(8,128)} %param.20) | copy-start | bytes 294916
  2.5 60.7 %all-to-all-start = ((s32[8,6,1]{1,2,0:T(1,128)}), s32[8,6,1]{1,2,0:T(1,128)S(1)}, u32[]{:S(2)}, u32[]{:S(2)}) async-start(s32[8,6,1]{1,2,0:T(1,128)} %bitcast.5), calls=%async_computation | async-start | bytes 8192 | tf_op jit(solution)/shard_map/all_to_all | solution.py:51
  16.7 25.8 %copy-start.1 = (f32[32,256]{1,0:T(8,128)S(1)}, f32[32,256]{1,0:T(8,128)}, u32[]{:S(2)}) copy-start(f32[32,256]{1,0:T(8,128)} %param.14) | copy-start | bytes 98308
  16.7 25.8 %copy-start.2 = (f32[32,256]{1,0:T(8,128)S(1)}, f32[32,256]{1,0:T(8,128)}, u32[]{:S(2)}) copy-start(f32[32,256]{1,0:T(8,128)} %param.15) | copy-start | bytes 98308
  51.9 25.5 %copy-start.5 = (s32[32]{0:T(128)S(1)}, s32[32]{0:T(128)}, u32[]{:S(2)}) copy-start(s32[32]{0:T(128)} %param.17) | copy-start | bytes 388
  51.9 66.6 %copy-start.3 = (f32[32]{0:T(128)S(1)}, f32[32]{0:T(128)}, u32[]{:S(2)}) copy-start(f32[32]{0:T(128)} %param.19) | copy-start | bytes 388
  63.2 13.8 %all-to-all-start.1 = ((f32[8,6,768]{2,1,0:T(8,128)}), f32[8,6,768]{2,1,0:T(8,128)S(1)}, u32[]{:S(2)}, u32[]{:S(2)}) async-start(f32[8,6,768]{2,1,0:T(8,128)} %fusion.42), calls=%async_computation.1 | async-start | bytes 393216 | tf_op jit(solution)/shard_map/all_to_all | solution.py:77
  77.3 38.8 %collective-permute-start = (f32[32,768]{1,0:T(8,128)S(1)}, f32[32,768]{1,0:T(8,128)S(1)}, u32[]{:S(2)}, u32[]{:S(2)}) collective-permute-start(f32[32,768]{1,0:T(8,128)S(1)} %fusion.33), channel_id=1, source_target_pairs={{0,1},{1,0},{2,3},{3,2},{4,5},{5,4},{6,7},{7,6},{8,9},{9,8},{10,11... | collective-permute-start | bytes 294920 | tf_op jit(solution)/shard_map/ppermute | solution.py:81
  116.1 4.9 %collective-permute-start.1 = (f32[32,768]{1,0:T(8,128)S(1)}, f32[32,768]{1,0:T(8,128)S(1)}, u32[]{:S(2)}, u32[]{:S(2)}) collective-permute-start(f32[32,768]{1,0:T(8,128)S(1)} %add.153), channel_id=1, source_target_pairs={{0,2},{1,3},{2,0},{3,1},{4,6},{5,7},{6,4},{7,5},{8,10},{9,11},{10,... | collective-permute-start | bytes 294920 | tf_op jit(solution)/shard_map/ppermute | solution.py:81
  122.1 12.2 %all-to-all-start.2 = ((f32[8,6,768]{2,1,0:T(8,128)}), f32[8,6,768]{2,1,0:T(8,128)S(1)}, u32[]{:S(2)}, u32[]{:S(2)}) async-start(f32[8,6,768]{2,1,0:T(8,128)} %all_to_all.77), calls=%async_computation.2 | async-start | bytes 393216 | tf_op jit(solution)/shard_map/all_to_all | solution.py:90
  186.3 1.4 collective-permute-start.2
  187.7 4.9 %collective-permute-start.3 = (f32[32,768]{1,0:T(8,128)S(1)}, f32[32,768]{1,0:T(8,128)S(1)}, u32[]{:S(2)}, u32[]{:S(2)}) collective-permute-start(f32[32,768]{1,0:T(8,128)S(1)} %add.159), channel_id=1, source_target_pairs={{0,2},{1,3},{2,0},{3,1},{4,6},{5,7},{6,4},{7,5},{8,10},{9,11},{10,... | collective-permute-start | bytes 294920 | tf_op jit(solution)/shard_map/ppermute | solution.py:81
  193.7 11.1 %all-to-all-start.4 = ((f32[8,6,768]{2,1,0:T(8,128)}), f32[8,6,768]{2,1,0:T(8,128)S(1)}, u32[]{:S(2)}, u32[]{:S(2)}) async-start(f32[8,6,768]{2,1,0:T(8,128)} %all_to_all.82), calls=%async_computation.4 | async-start | bytes 393216 | tf_op jit(solution)/shard_map/all_to_all | solution.py:90
  256.9 1.4 collective-permute-start.4
  258.3 4.9 %collective-permute-start.5 = (f32[32,768]{1,0:T(8,128)S(1)}, f32[32,768]{1,0:T(8,128)S(1)}, u32[]{:S(2)}, u32[]{:S(2)}) collective-permute-start(f32[32,768]{1,0:T(8,128)S(1)} %add.164), channel_id=1, source_target_pairs={{0,2},{1,3},{2,0},{3,1},{4,6},{5,7},{6,4},{7,5},{8,10},{9,11},{10,... | collective-permute-start | bytes 294920 | tf_op jit(solution)/shard_map/ppermute | solution.py:81
  264.2 11.1 %all-to-all-start.6 = ((f32[8,6,768]{2,1,0:T(8,128)}), f32[8,6,768]{2,1,0:T(8,128)S(1)}, u32[]{:S(2)}, u32[]{:S(2)}) async-start(f32[8,6,768]{2,1,0:T(8,128)} %all_to_all.87), calls=%async_computation.6 | async-start | bytes 393216 | tf_op jit(solution)/shard_map/all_to_all | solution.py:90
  327.6 1.4 collective-permute-start.6
  329.0 4.9 %collective-permute-start.7 = (f32[32,768]{1,0:T(8,128)S(1)}, f32[32,768]{1,0:T(8,128)S(1)}, u32[]{:S(2)}, u32[]{:S(2)}) collective-permute-start(f32[32,768]{1,0:T(8,128)S(1)} %add.169), channel_id=1, source_target_pairs={{0,2},{1,3},{2,0},{3,1},{4,6},{5,7},{6,4},{7,5},{8,10},{9,11},{10,... | collective-permute-start | bytes 294920 | tf_op jit(solution)/shard_map/ppermute | solution.py:81
  335.0 11.1 %all-to-all-start.8 = ((f32[8,6,768]{2,1,0:T(8,128)}), f32[8,6,768]{2,1,0:T(8,128)S(1)}, u32[]{:S(2)}, u32[]{:S(2)}) async-start(f32[8,6,768]{2,1,0:T(8,128)} %all_to_all.92), calls=%async_computation.8 | async-start | bytes 393216 | tf_op jit(solution)/shard_map/all_to_all | solution.py:90
  397.2 1.4 collective-permute-start.8
  398.5 4.9 %collective-permute-start.9 = (f32[32,768]{1,0:T(8,128)S(1)}, f32[32,768]{1,0:T(8,128)S(1)}, u32[]{:S(2)}, u32[]{:S(2)}) collective-permute-start(f32[32,768]{1,0:T(8,128)S(1)} %add.174), channel_id=1, source_target_pairs={{0,2},{1,3},{2,0},{3,1},{4,6},{5,7},{6,4},{7,5},{8,10},{9,11},{10,... | collective-permute-start | bytes 294920 | tf_op jit(solution)/shard_map/ppermute | solution.py:81
  405.3 12.9 %all-to-all-start.10 = ((f32[8,6,768]{2,1,0:T(8,128)}), f32[8,6,768]{2,1,0:T(8,128)S(1)}, u32[]{:S(2)}, u32[]{:S(2)}) async-start(f32[8,6,768]{2,1,0:T(8,128)} %all_to_all.97), calls=%async_computation.10 | async-start | bytes 393216 | tf_op jit(solution)/shard_map/all_to_all | solution.py:90
  408.7 61.5 %copy-start.4 = (f32[2]{0:T(128)S(1)}, f32[2]{0:T(128)}, u32[]{:S(2)}) copy-start(f32[2]{0:T(128)} %constant.68.clone) | copy-start | bytes 28
